TPU v7x, 256 devices: a whole 4x4x8 slice. The times are simulated.
256 devices in a mesh: dp: 8 (over z_lo, core), expert: 32 (over y, x, z_hi).
Axes of the slice: x: 4, y: 4, z: 8 (z_hi: 2, z_lo: 4; z = z_hi * 4 + z_lo), core: 2. Of those that a mesh axis runs over, the one named last changes fastest.
Arguments:
- tokens: bfloat16 [32768, 3584], P(('dp', 'expert')), may hold values from -6 to 6
- cotangent: bfloat16 [32768, 3584], P(('dp', 'expert')), may hold values from -6 to 6
- gates: float32 [32768, 1], P(('dp', 'expert')), may hold values from 0.1 to 1
- routes: int32 [32768, 1], P(('dp', 'expert')), may hold values from 0 to 31; in each aligned block of 128 rows (0 to 127, 128 to 255, ...) at most 5 rows name the same one
- w_up: bfloat16 [32, 3584, 1024], P('expert', None, 'dp'), may hold values from -0.09375 to 0.09375
- w_down: bfloat16 [32, 1024, 3584], P('expert', 'dp'), may hold values from -0.1875 to 0.1875
- m_up: bfloat16 [32, 3584, 1024], P('expert', None, 'dp'), may hold values from -3 to 3
- v_up: bfloat16 [32, 3584, 1024], P('expert', None, 'dp'), may hold values from 0.099609375 to 1
- m_down: bfloat16 [32, 1024, 3584], P('expert', 'dp'), may hold values from -3 to 3
- v_down: bfloat16 [32, 1024, 3584], P('expert', 'dp'), may hold values from 0.099609375 to 1
- leaving: int32 [1], replicated, may hold values from 0 to 31
- tile_owner: int32 [32], replicated, may hold values from 0 to 31, each once
Outputs:
- update_up: bfloat16 [32, 3584, 1024], P('expert', None, 'dp')
- update_down: bfloat16 [32, 1024, 3584], P('expert', 'dp')
- adopted_up: bfloat16 [32, 112, 1024], P('expert', None, 'dp')
- adopted_down: bfloat16 [32, 112, 1024], P('expert', None, 'dp')
Inputs may be any that keep to these rules, and one draw needn't show every extreme that they name: `routes`: each row names one expert; within the 128 rows of one device no expert is named more than 5 times, a bound that some block reaches in some devices. `tile_owner`: A permutation of the 32 device indices of the expert axis.
All inputs are finite; a program needn't handle non-finite values.
Results may differ from a plain program's by a relative error of at most 0.0041.
Values may be sent and summed in bfloat16 or wider, within the bound.
A program may use at most 128 MiB of HBM per device.

v0:
```python
import jax
import jax.numpy as jnp
from jax import lax
from jax.sharding import PartitionSpec as P

BETA_ONE = 0.9
BETA_TWO = 0.95
EPSILON = 1e-08


def expert_terms(rows_x, rows_c, up_tile, down_tile):
    preact = jnp.dot(rows_x, up_tile, preferred_element_type=jnp.float32)
    squash = jax.nn.sigmoid(preact)
    hidden = (preact * squash).astype(jnp.bfloat16)
    slope_val = squash * (1.0 + preact * (1.0 - squash))
    back_grad = lax.dot_general(
        rows_c, down_tile, (((1,), (1,)), ((), ())), preferred_element_type=jnp.float32
    )
    pre_grad = (back_grad * slope_val).astype(jnp.bfloat16)
    grad_up = lax.dot_general(
        rows_x, pre_grad, (((0,), (0,)), ((), ())), preferred_element_type=jnp.float32
    )
    grad_cols = lax.dot_general(
        rows_c, hidden, (((0,), (0,)), ((), ())), preferred_element_type=jnp.float32
    )
    return (grad_up, grad_cols)


def adam_step(gradient, moment_one, moment_two):
    new_one = BETA_ONE * moment_one.astype(jnp.float32) + (1.0 - BETA_ONE) * gradient
    new_two = BETA_TWO * moment_two.astype(jnp.float32) + (1.0 - BETA_TWO) * gradient * gradient
    return (new_one / (jnp.sqrt(new_two) + EPSILON)).astype(jnp.bfloat16)


def on_device(
    tokens, cotangent, gates, routes, w_up, w_down, m_up, v_up, m_down, v_down, leaving, tile_owner
):
    experts = lax.axis_size("expert")
    my_index = lax.axis_index("expert")
    tok_count, model_width = tokens.shape
    top_count = routes.shape[1]
    hidden_units = w_up.shape[2]
    capacity = 5 * tok_count * top_count // (4 * experts)
    pair_count = tok_count * top_count
    leaver = leaving[0]
    slot_ids = jnp.arange(experts, dtype=jnp.int32)
    tile_rows = model_width // experts
    adopt = jnp.sum(
        jnp.where(tile_owner[None, :] == slot_ids[:, None], slot_ids[None, :], 0), axis=1
    )
    expert_of = routes.reshape(pair_count)
    member = (expert_of[:, None] == slot_ids[None, :]).astype(jnp.int32)
    slot_rank = jnp.sum((jnp.cumsum(member, axis=0) - 1) * member, axis=1)
    slot_place = expert_of * capacity + slot_rank
    staying = expert_of != leaver
    send_mask = jnp.ones_like(staying)
    pair_x = jnp.repeat(tokens, top_count, axis=0)
    pair_c = (
        gates.reshape(pair_count)[:, None]
        * jnp.repeat(cotangent, top_count, axis=0).astype(jnp.float32)
    ).astype(jnp.bfloat16)
    pair_both = jnp.concatenate([pair_x, pair_c], axis=1)
    targets = jnp.arange(experts * capacity, dtype=jnp.int32)
    picker = ((slot_place[None, :] == targets[:, None]) & send_mask[None, :]).astype(jnp.bfloat16)
    send_both = jnp.dot(picker, pair_both, preferred_element_type=jnp.float32).astype(jnp.bfloat16)
    send_x = send_both[:, :model_width].reshape(experts, capacity, model_width)
    send_c = send_both[:, model_width:].reshape(experts, capacity, model_width)
    recv_x, recv_c = (
        lax.all_to_all(send_x, "expert", split_axis=0, concat_axis=0, tiled=True),
        lax.all_to_all(send_c, "expert", split_axis=0, concat_axis=0, tiled=True),
    )
    recv_x = recv_x.reshape(experts * capacity, model_width)
    recv_c = recv_c.reshape(experts * capacity, model_width)
    grad_up, grad_cols = expert_terms(
        lax.all_gather(recv_x, "dp", axis=0, tiled=True),
        lax.all_gather(recv_c, "dp", axis=0, tiled=True),
        w_up[0],
        w_down[0],
    )
    keep_own = my_index != leaver
    step_up = adam_step(grad_up, m_up[0], v_up[0])
    step_down = adam_step(grad_cols.T, m_down[0], v_down[0])
    both_steps = jnp.concatenate([step_up, step_down.T], axis=1).reshape(
        experts, tile_rows, 2 * hidden_units
    )
    ordered = both_steps[adopt]
    outgoing = jnp.where(keep_own, jnp.zeros_like(ordered), ordered)
    incoming = lax.all_to_all(outgoing, "expert", split_axis=0, concat_axis=0, tiled=True)
    mine = lax.dynamic_index_in_dim(incoming, leaver, 0, keepdims=False)
    adopted_up = mine[:, :hidden_units][None]
    adopted_down = mine[:, hidden_units:][None]
    update_up = jnp.where(keep_own, step_up, jnp.zeros_like(step_up))[None]
    update_down = jnp.where(keep_own, step_down, jnp.zeros_like(step_down))[None]
    return (update_up, update_down, adopted_up, adopted_down)


def solution(mesh):
    placed = (
        P(("dp", "expert"), None),
        P(("dp", "expert"), None),
        P(("dp", "expert"), None),
        P(("dp", "expert"), None),
        P("expert", None, "dp"),
        P("expert", "dp", None),
        P("expert", None, "dp"),
        P("expert", None, "dp"),
        P("expert", "dp", None),
        P("expert", "dp", None),
        P(),
        P(),
    )
    return jax.shard_map(
        on_device,
        mesh=mesh,
        in_specs=placed,
        out_specs=(
            P("expert", None, "dp"),
            P("expert", "dp", None),
            P("expert", None, "dp"),
            P("expert", None, "dp"),
        ),
        check_vma=False,
    )
```

profile of v0, /device:TPU:33, one launch (start us, length us, event | category | flops | bytes accessed | tf_op | source)
XLA Modules:
  0.0 402.2 jit_solution(538637933655754063)
XLA Ops:
  7.2 0.0 copy-start
  7.2 0.0 copy-start.7
  7.2 0.0 all-gather.3.cloned.1.call-start
  7.2 0.9 fusion.19
  8.1 0.2 reduce_window_sum.11
  8.3 0.8 select_reduce_fusion
  9.1 0.7 multiply_add_fusion
  9.8 1.4 multiply_convert_fusion
  11.2 0.0 copy-done.7
  11.2 0.7 convolution_convert_fusion
  11.9 1.5 fusion.25
  13.5 1.5 reshape.61
  15.0 61.8 %all_to_all.15 = bf16[32,5,3584]{2,1,0:T(8,128)(2,1)} all-to-all(bf16[32,5,3584]{2,1,0:T(8,128)(2,1)S(1)} %reshape.61), channel_id=1, replica_groups=mesh['dp'=8,'expert'=32] {'expert'}, dimensions={0} | all-to-all | bytes 2293760 | tf_op jit(solution)/shard_map/all_to_all | solution.py:69
  76.8 2.5 reshape.62
  79.3 0.0 all-gather.3.cloned.1.call-update
  79.3 0.0 all-gather.5.cloned.1.call-start
  79.4 1.5 reshape.63
  80.9 62.4 %all_to_all.16 = bf16[32,5,3584]{2,1,0:T(8,128)(2,1)} all-to-all(bf16[32,5,3584]{2,1,0:T(8,128)(2,1)S(1)} %reshape.63), channel_id=1, replica_groups=mesh['dp'=8,'expert'=32] {'expert'}, dimensions={0} | all-to-all | bytes 2293760 | tf_op jit(solution)/shard_map/all_to_all | solution.py:70
  143.4 2.6 reshape.64
  146.0 0.0 all-gather.5.cloned.1.call-update
  146.7 0.0 copy-done.2
  146.7 0.0 copy-start.9
  146.7 1.3 copy.24
  148.0 0.0 copy-done.3
  148.0 1.3 copy.25
  149.3 0.0 copy-done.9
  149.3 0.1 select_reduce_fusion.1
  149.4 52.1 %all-gather.3.cloned.1.call-done = bf16[1280,3584]{1,0:T(8,128)(2,1)} async-done(((bf16[160,3584]{1,0:T(8,128)(2,1)}), bf16[1280,3584]{1,0:T(8,128)(2,1)}) %all-gather.3.cloned.1.call-update) | async-done | bytes 9175056 | tf_op jit(solution)/shard_map/all_gather | solution.py:75
  201.5 0.0 copy-done.8
  201.5 6.2 %fusion.14 = f32[1280,128]{1,0:T(8,128)S(1)} fusion(bf16[1280,3584]{1,0:T(8,128)(2,1)} %all-gather.3.cloned.1.call-done, bf16[1,3584,128]{2,1,0:T(8,128)(2,1)S(1)} %copy-done.8), kind=kOutput, calls=%fused_computation.24 | convolution fusion | flops 1174405120 | bytes 10747904 | tf_op jit(solution)/shard_map/dot_general | solution.py:12
  207.7 0.0 copy-start.5
  207.7 0.0 copy-start.6
  207.7 96.3 %all-gather.5.cloned.1.call-done = bf16[1280,3584]{1,0:T(8,128)(2,1)} async-done(((bf16[160,3584]{1,0:T(8,128)(2,1)}), bf16[1280,3584]{1,0:T(8,128)(2,1)}) %all-gather.5.cloned.1.call-update) | async-done | bytes 9175056 | tf_op jit(solution)/shard_map/all_gather | solution.py:76
  304.0 7.4 %fusion.12 = bf16[128,3584]{1,0:T(8,128)(2,1)} fusion(bf16[1,128,3584]{2,1,0:T(8,128)(2,1)} %param.21, bf16[1,128,3584]{2,1,0:T(8,128)(2,1)} %param.20, bf16[1280,3584]{1,0:T(8,128)(2,1)} %all-gather.5.cloned.1.call-done, f32[1280,128]{1,0:T(8,128)S(1)} %fusion.14), kind=kOutput, calls=%fused_computation.21 | convolution fusion | flops 1180729344 | bytes 12582912 | tf_op jit(solution)/shard_map/dot_general | solution.py:23
  311.4 0.0 copy-done
  311.4 0.0 copy-done.5
  311.4 0.0 copy-done.6
  311.4 14.3 %select_bitcast_fusion.1 = (bf16[1,3584,128]{1,2,0:T(8,128)(2,1)}, bf16[3584,128]{0,1:T(8,128)(2,1)}) fusion(pred[]{:T(512)S(6)} %ne.3, bf16[1,3584,128]{1,2,0:T(8,128)(2,1)S(1)} %copy-done.6, bf16[1,3584,128]{1,2,0:T(8,128)(2,1)S(1)} %copy-done.5, bf16[1280,3584]{1,0:T(8,128)(2,1)} %all-gather.3.cloned.1.call-done, ...), kind=kOutput, calls=%fused_computation.28 | convolution fusion | flops 2356248576 | bytes 23592960 | tf_op jit(solution)/shard_map/dot_general | solution.py:20
  325.7 1.6 pad_maximum_fusion
  327.3 2.3 copy.26
  329.6 2.2 gather_fusion
  331.7 1.4 broadcast_select_fusion
  333.1 10.5 %all-to-all-start.2 = ((bf16[32,112,256]{2,1,0:T(8,128)(2,1)}), bf16[32,112,256]{2,1,0:T(8,128)(2,1)}, u32[]{:S(2)}, u32[]{:S(2)}) async-start(bf16[32,112,256]{2,1,0:T(8,128)(2,1)} %broadcast_select_fusion), calls=%async_computation.2 | async-start | bytes 3670016 | tf_op jit(solution)/shard_map/all_to_all | solution.py:88
  343.6 1.3 copy.27
  344.9 1.0 select_bitcast_fusion
  345.9 48.0 %all-to-all-done.2 = bf16[32,112,256]{2,1,0:T(8,128)(2,1)} async-done(((bf16[32,112,256]{2,1,0:T(8,128)(2,1)}), bf16[32,112,256]{2,1,0:T(8,128)(2,1)}, u32[]{:S(2)}, u32[]{:S(2)}) %all-to-all-start.2) | async-done | bytes 1835040 | tf_op jit(solution)/shard_map/all_to_all | solution.py:88
  393.9 0.8 dynamic-slice_bitcast_fusion
  394.7 0.6 slice_bitcast_fusion
  (9 shorter events, 0.0 us)
Async XLA Ops:
  7.2 304.2 %copy-start = (bf16[1,128,3584]{2,1,0:T(8,128)(2,1)S(1)}, bf16[1,128,3584]{2,1,0:T(8,128)(2,1)}, u32[]{:S(2)}) copy-start(bf16[1,128,3584]{2,1,0:T(8,128)(2,1)} %param.17) | copy-start | bytes 2752516
  7.2 4.0 copy-start.7
  7.2 194.3 %all-gather.3.cloned.1.call-start = ((), (), s32[]{:S(2)}) async-start(), calls=%async_computation.3 | async-start | bytes 10321920 | tf_op jit(solution)/shard_map/all_gather | solution.py:75
  79.3 224.6 %all-gather.5.cloned.1.call-start = ((), (), s32[]{:S(2)}) async-start(), calls=%async_computation.4 | async-start | bytes 10321920 | tf_op jit(solution)/shard_map/all_gather | solution.py:76
  143.3 3.4 copy-start.2
  146.0 2.1 copy-start.3
  146.7 2.6 copy-start.9
  148.0 53.5 %copy-start.8 = (bf16[1,3584,128]{2,1,0:T(8,128)(2,1)S(1)}, bf16[1,3584,128]{2,1,0:T(8,128)(2,1)}, u32[]{:S(2)}) copy-start(bf16[1,3584,128]{2,1,0:T(8,128)(2,1)} %param.16) | copy-start | bytes 2752516
  207.7 103.7 %copy-start.5 = (bf16[1,3584,128]{1,2,0:T(8,128)(2,1)S(1)}, bf16[1,3584,128]{1,2,0:T(8,128)(2,1)}, u32[]{:S(2)}) copy-start(bf16[1,3584,128]{1,2,0:T(8,128)(2,1)} %copy.24) | copy-start | bytes 2752516
  207.7 103.7 %copy-start.6 = (bf16[1,3584,128]{1,2,0:T(8,128)(2,1)S(1)}, bf16[1,3584,128]{1,2,0:T(8,128)(2,1)}, u32[]{:S(2)}) copy-start(bf16[1,3584,128]{1,2,0:T(8,128)(2,1)} %copy.25) | copy-start | bytes 2752516
  333.1 10.5 %copy-start.4 = (bf16[1,3584,128]{1,2,0:T(8,128)(2,1)S(1)}, bf16[1,3584,128]{1,2,0:T(8,128)(2,1)}, u32[]{:S(2)}) copy-start(bf16[1,3584,128]{1,2,0:T(8,128)(2,1)} %get-tuple-element.16) | copy-start | bytes 2752516
  333.1 60.8 %all-to-all-start.2 = ((bf16[32,112,256]{2,1,0:T(8,128)(2,1)}), bf16[32,112,256]{2,1,0:T(8,128)(2,1)}, u32[]{:S(2)}, u32[]{:S(2)}) async-start(bf16[32,112,256]{2,1,0:T(8,128)(2,1)} %broadcast_select_fusion), calls=%async_computation.2 | async-start | bytes 3670016 | tf_op jit(solution)/shard_map/all_to_all | solution.py:88
  343.6 1.3 copy-start.1
Sparse Core Ops, SparseCore 0:
  79.5 122.0 all-gather.2
  203.3 100.6 all-gather.4
where the time goes:
time: 403 us; the launch traced here: 402 us
  waiting for transfers between devices  196 us (49%)
  blocking collectives  124 us (31%)
  matrix products  28.6 us (7%)
  local copies, waits for them, and re-layouts  19.5 us (5%)
  between operations  14.9 us (4%)
  starting transfers between devices  10.6 us (3%)
  other arithmetic  7.97 us (2%)
    all_gather x1, waiting for transfers between devices, on_device(): lax.all_gather(recv_c, 'dp', axis=0, tiled=True)  96.3 us
    all_to_all x1, blocking collectives, on_device(): lax.all_to_all(send_c, 'expert', split_axis=0, concat_axis=0, tiled=True)  62.4 us
    all_to_all x1, blocking collectives, on_device(): lax.all_to_all(send_x, 'expert', split_axis=0, concat_axis=0, tiled=True)  61.8 us
    all_gather x1, waiting for transfers between devices, on_device(): lax.all_gather(recv_x, 'dp', axis=0, tiled=True)  52.1 us
    all_to_all x1, waiting for transfers between devices, on_device(): lax.all_to_all(outgoing, 'expert', split_axis=0, concat_axis=0, tiled=True)  48 us
    dot_general x1, matrix products, expert_terms(): lax.dot_general(rows_x, pre_grad, (((0,), (0,)), ((), ())), preferred_ele...  14.3 us
    all_to_all x1, starting transfers between devices, on_device(): lax.all_to_all(outgoing, 'expert', split_axis=0, concat_axis=0, tiled=True)  10.5 us
  transfers between devices with their start and end apart: 3, of which 3 were waited for; matrix products, arithmetic and copies ran while one was open for 4% of the time, Pallas kernels for 0%

commit v1 on v0

--- a/solution.py
+++ b/solution.py
@@ -73,7 +73,9 @@
     recv_c = recv_c.reshape(experts * capacity, model_width)
     grad_up, grad_cols = expert_terms(
         lax.all_gather(recv_x, "dp", axis=0, tiled=True),
-        lax.all_gather(recv_c, "dp", axis=0, tiled=True),
+        jnp.concatenate(
+            lax.all_to_all(jnp.stack([recv_c] * lax.axis_size("dp")), "dp", 0, 0), axis=0
+        ),
         w_up[0],
         w_down[0],
     )

time: 403 us -> 494 us (1.23)
  the two profiles are of different devices: /device:TPU:33 before, /device:TPU:1 now
where the time goes in v1:
time: 494 us; the launch traced here: 493 us
  waiting for transfers between devices  341 us (69%)
  starting transfers between devices  74.4 us (15%)
  matrix products  28.8 us (6%)
  local copies, waits for them, and re-layouts  25.7 us (5%)
  between operations  14.9 us (3%)
  other arithmetic  7.97 us (2%)
    all_gather x1, waiting for transfers between devices, on_device(): lax.all_gather(recv_x, 'dp', axis=0, tiled=True)  147 us
    all_to_all x1, waiting for transfers between devices, on_device(): lax.all_to_all(jnp.stack([recv_c] * lax.axis_size('dp')), 'dp', 0, 0)  99.8 us
    all_to_all x1, starting transfers between devices, on_device(): lax.all_to_all(jnp.stack([recv_c] * lax.axis_size('dp')), 'dp', 0, 0)  47.7 us
    all_to_all x1, waiting for transfers between devices, on_device(): lax.all_to_all(outgoing, 'expert', split_axis=0, concat_axis=0, tiled=True)  44.2 us
    all_to_all x1, waiting for transfers between devices, on_device(): lax.all_to_all(send_x, 'expert', split_axis=0, concat_axis=0, tiled=True)  31.6 us
    all_to_all x1, waiting for transfers between devices, on_device(): lax.all_to_all(send_c, 'expert', split_axis=0, concat_axis=0, tiled=True)  19.1 us
    all_to_all x1, starting transfers between devices, on_device(): lax.all_to_all(send_x, 'expert', split_axis=0, concat_axis=0, tiled=True)  14.5 us
    dot_general x1, matrix products, expert_terms(): lax.dot_general(rows_x, pre_grad, (((0,), (0,)), ((), ())), preferred_ele...  14.3 us
  transfers between devices with their start and end apart: 5, of which 5 were waited for; matrix products, arithmetic and copies ran while one was open for 5% of the time, Pallas kernels for 0%

profile of v1, /device:TPU:1, one launch (start us, length us, event | category | flops | bytes accessed | tf_op | source)
XLA Modules:
  0.0 493.3 jit_solution(416708973883627467)
XLA Ops:
  7.2 0.0 copy-start
  7.2 0.0 copy-start.8
  7.2 0.9 fusion.19
  8.1 0.2 reduce_window_sum.11
  8.2 0.8 select_reduce_fusion
  9.1 0.7 multiply_add_fusion
  9.7 1.4 multiply_convert_fusion
  11.1 0.0 copy-done.8
  11.1 0.7 convolution_convert_fusion
  11.9 1.2 fusion.25
  13.1 1.5 reshape.63
  14.6 14.5 %all-to-all-start = ((bf16[32,5,3584]{2,1,0:T(8,128)(2,1)}), bf16[32,5,3584]{2,1,0:T(8,128)(2,1)S(1)}, u32[]{:S(2)}, u32[]{:S(2)}) async-start(bf16[32,5,3584]{2,1,0:T(8,128)(2,1)} %reshape.63), calls=%async_computation | async-start | bytes 3670016 | tf_op jit(solution)/shard_map/all_to_all | solution.py:69
  29.1 2.5 reshape.65
  31.6 31.6 %all-to-all-done = bf16[32,5,3584]{2,1,0:T(8,128)(2,1)S(1)} async-done(((bf16[32,5,3584]{2,1,0:T(8,128)(2,1)}), bf16[32,5,3584]{2,1,0:T(8,128)(2,1)S(1)}, u32[]{:S(2)}, u32[]{:S(2)}) %all-to-all-start) | async-done | bytes 1146912 | tf_op jit(solution)/shard_map/all_to_all | solution.py:69
  63.2 1.3 copy-done.1
  64.4 4.0 all-to-all-start.1
  68.4 0.0 all-gather.2.cloned.1.call-start
  68.5 2.5 reshape.64
  71.0 0.0 all-gather.2.cloned.1.call-update
  71.0 19.1 %all-to-all-done.1 = bf16[32,5,3584]{2,1,0:T(8,128)(2,1)S(1)} async-done(((bf16[32,5,3584]{2,1,0:T(8,128)(2,1)}), bf16[32,5,3584]{2,1,0:T(8,128)(2,1)S(1)}, u32[]{:S(2)}, u32[]{:S(2)}) %all-to-all-start.1) | async-done | bytes 1146912 | tf_op jit(solution)/shard_map/all_to_all | solution.py:70
  90.1 1.3 stack_reshape.2
  91.3 5.6 %stack.3 = bf16[8,160,3584]{2,1,0:T(8,128)(2,1)} broadcast(bf16[160,3584]{1,0:T(8,128)(2,1)} %stack_reshape.2), dimensions={1,2} | broadcast | bytes 10321920 | tf_op jit(solution)/shard_map/stack | solution.py:77
  97.0 47.7 %all-to-all-start.2 = ((bf16[8,160,3584]{2,1,0:T(8,128)(2,1)}), bf16[8,160,3584]{2,1,0:T(8,128)(2,1)}, u32[]{:S(2)}, u32[]{:S(2)}) async-start(bf16[8,160,3584]{2,1,0:T(8,128)(2,1)} %stack.3), calls=%async_computation.2 | async-start | bytes 18350080 | tf_op jit(solution)/shard_map/all_to_all | solution.py:77
  145.4 0.0 copy-done.3
  145.4 0.0 copy-start.10
  145.4 1.3 copy.24
  146.7 0.0 copy-done.4
  146.7 1.3 copy.25
  148.0 0.0 copy-done.10
  148.0 0.1 select_reduce_fusion.1
  148.1 146.8 %all-gather.2.cloned.1.call-done = bf16[1280,3584]{1,0:T(8,128)(2,1)} async-done(((bf16[160,3584]{1,0:T(8,128)(2,1)}), bf16[1280,3584]{1,0:T(8,128)(2,1)}) %all-gather.2.cloned.1.call-update) | async-done | bytes 9175056 | tf_op jit(solution)/shard_map/all_gather | solution.py:75
  294.9 0.0 copy-done.9
  294.9 6.2 %fusion.14 = f32[1280,128]{1,0:T(8,128)S(1)} fusion(bf16[1280,3584]{1,0:T(8,128)(2,1)} %all-gather.2.cloned.1.call-done, bf16[1,3584,128]{2,1,0:T(8,128)(2,1)S(1)} %copy-done.9), kind=kOutput, calls=%fused_computation.24 | convolution fusion | flops 1174405120 | bytes 10747904 | tf_op jit(solution)/shard_map/dot_general | solution.py:12
  301.1 99.8 %all-to-all-done.2 = bf16[8,160,3584]{2,1,0:T(8,128)(2,1)} async-done(((bf16[8,160,3584]{2,1,0:T(8,128)(2,1)}), bf16[8,160,3584]{2,1,0:T(8,128)(2,1)}, u32[]{:S(2)}, u32[]{:S(2)}) %all-to-all-start.2) | async-done | bytes 9175072 | tf_op jit(solution)/shard_map/all_to_all | solution.py:77
  400.9 7.6 %fusion.12 = bf16[128,3584]{1,0:T(8,128)(2,1)} fusion(bf16[1,128,3584]{2,1,0:T(8,128)(2,1)} %param.21, bf16[1,128,3584]{2,1,0:T(8,128)(2,1)} %param.20, bf16[1280,3584]{1,0:T(8,128)(2,1)} %bitcast.4, f32[1280,128]{1,0:T(8,128)S(1)} %fusion.14), kind=kOutput, calls=%fused_computation.21 | convolution fusion | flops 1180729344 | bytes 12582912 | tf_op jit(solution)/shard_map/dot_general | solution.py:23
  408.5 0.0 copy-done
  408.5 0.0 copy-done.6
  408.5 14.3 %select_bitcast_fusion.1 = (bf16[1,3584,128]{1,2,0:T(8,128)(2,1)}, bf16[3584,128]{0,1:T(8,128)(2,1)}) fusion(pred[]{:T(512)S(6)} %ne.3, bf16[1,3584,128]{1,2,0:T(8,128)(2,1)S(1)} %copy-done.7, bf16[1,3584,128]{1,2,0:T(8,128)(2,1)S(1)} %copy-done.6, bf16[1280,3584]{1,0:T(8,128)(2,1)} %all-gather.2.cloned.1.call-done, bf16[1280,3584]{1,0:T(8,128)(2,1)} %bitcast.4, ...), kind=kOutput, calls=%fused_computation.28 | convolution fusion | flops 2356248576 | bytes 23592960 | tf_op jit(solution)/shard_map/dot_general | solution.py:20
  422.8 1.6 pad_maximum_fusion
  424.4 2.3 copy.26
  426.7 2.2 gather_fusion
  428.9 1.4 broadcast_select_fusion
  430.2 8.3 %all-to-all-start.3 = ((bf16[32,112,256]{2,1,0:T(8,128)(2,1)}), bf16[32,112,256]{2,1,0:T(8,128)(2,1)}, u32[]{:S(2)}, u32[]{:S(2)}) async-start(bf16[32,112,256]{2,1,0:T(8,128)(2,1)} %broadcast_select_fusion), calls=%async_computation.3 | async-start | bytes 3670016 | tf_op jit(solution)/shard_map/all_to_all | solution.py:90
  438.5 1.3 copy.27
  439.8 1.0 select_bitcast_fusion
  440.8 44.2 %all-to-all-done.3 = bf16[32,112,256]{2,1,0:T(8,128)(2,1)} async-done(((bf16[32,112,256]{2,1,0:T(8,128)(2,1)}), bf16[32,112,256]{2,1,0:T(8,128)(2,1)}, u32[]{:S(2)}, u32[]{:S(2)}) %all-to-all-start.3) | async-done | bytes 1835040 | tf_op jit(solution)/shard_map/all_to_all | solution.py:90
  485.0 0.8 dynamic-slice_bitcast_fusion
  485.8 0.6 slice_bitcast_fusion
  (13 shorter events, 0.0 us)
Async XLA Ops:
  7.2 401.4 %copy-start = (bf16[1,128,3584]{2,1,0:T(8,128)(2,1)S(1)}, bf16[1,128,3584]{2,1,0:T(8,128)(2,1)}, u32[]{:S(2)}) copy-start(bf16[1,128,3584]{2,1,0:T(8,128)(2,1)} %param.17) | copy-start | bytes 2752516
  7.2 4.0 copy-start.8
  14.6 48.6 %all-to-all-start = ((bf16[32,5,3584]{2,1,0:T(8,128)(2,1)}), bf16[32,5,3584]{2,1,0:T(8,128)(2,1)S(1)}, u32[]{:S(2)}, u32[]{:S(2)}) async-start(bf16[32,5,3584]{2,1,0:T(8,128)(2,1)} %reshape.63), calls=%async_computation | async-start | bytes 3670016 | tf_op jit(solution)/shard_map/all_to_all | solution.py:69
  63.2 1.3 copy-start.1
  64.4 25.6 %all-to-all-start.1 = ((bf16[32,5,3584]{2,1,0:T(8,128)(2,1)}), bf16[32,5,3584]{2,1,0:T(8,128)(2,1)S(1)}, u32[]{:S(2)}, u32[]{:S(2)}) async-start(bf16[32,5,3584]{2,1,0:T(8,128)(2,1)} %reshape.65), calls=%async_computation.1 | async-start | bytes 3670016 | tf_op jit(solution)/shard_map/all_to_all | solution.py:70
  68.4 226.5 %all-gather.2.cloned.1.call-start = ((), (), s32[]{:S(2)}) async-start(), calls=%async_computation.4 | async-start | bytes 10321920 | tf_op jit(solution)/shard_map/all_gather | solution.py:75
  97.0 48.4 %copy-start.3 = (bf16[1,3584,128]{2,1,0:T(8,128)(2,1)S(1)}, bf16[1,3584,128]{2,1,0:T(8,128)(2,1)}, u32[]{:S(2)}) copy-start(bf16[1,3584,128]{2,1,0:T(8,128)(2,1)} %param.18) | copy-start | bytes 2752516
  97.0 304.0 %all-to-all-start.2 = ((bf16[8,160,3584]{2,1,0:T(8,128)(2,1)}), bf16[8,160,3584]{2,1,0:T(8,128)(2,1)}, u32[]{:S(2)}, u32[]{:S(2)}) async-start(bf16[8,160,3584]{2,1,0:T(8,128)(2,1)} %stack.3), calls=%async_computation.2 | async-start | bytes 18350080 | tf_op jit(solution)/shard_map/all_to_all | solution.py:77
  144.7 2.0 copy-start.4
  145.4 2.6 copy-start.10
  146.7 148.2 %copy-start.9 = (bf16[1,3584,128]{2,1,0:T(8,128)(2,1)S(1)}, bf16[1,3584,128]{2,1,0:T(8,128)(2,1)}, u32[]{:S(2)}) copy-start(bf16[1,3584,128]{2,1,0:T(8,128)(2,1)} %param.16) | copy-start | bytes 2752516
  400.9 7.6 %copy-start.6 = (bf16[1,3584,128]{1,2,0:T(8,128)(2,1)S(1)}, bf16[1,3584,128]{1,2,0:T(8,128)(2,1)}, u32[]{:S(2)}) copy-start(bf16[1,3584,128]{1,2,0:T(8,128)(2,1)} %copy.24) | copy-start | bytes 2752516
  400.9 7.6 %copy-start.7 = (bf16[1,3584,128]{1,2,0:T(8,128)(2,1)S(1)}, bf16[1,3584,128]{1,2,0:T(8,128)(2,1)}, u32[]{:S(2)}) copy-start(bf16[1,3584,128]{1,2,0:T(8,128)(2,1)} %copy.25) | copy-start | bytes 2752516
  430.2 8.3 %copy-start.5 = (bf16[1,3584,128]{1,2,0:T(8,128)(2,1)S(1)}, bf16[1,3584,128]{1,2,0:T(8,128)(2,1)}, u32[]{:S(2)}) copy-start(bf16[1,3584,128]{1,2,0:T(8,128)(2,1)} %get-tuple-element.16) | copy-start | bytes 2752516
  430.2 54.7 %all-to-all-start.3 = ((bf16[32,112,256]{2,1,0:T(8,128)(2,1)}), bf16[32,112,256]{2,1,0:T(8,128)(2,1)}, u32[]{:S(2)}, u32[]{:S(2)}) async-start(bf16[32,112,256]{2,1,0:T(8,128)(2,1)} %broadcast_select_fusion), calls=%async_computation.3 | async-start | bytes 3670016 | tf_op jit(solution)/shard_map/all_to_all | solution.py:90
  438.5 1.3 copy-start.2
Sparse Core Ops, SparseCore 0:
  71.1 223.7 all-gather.1
